TPU v7x, 32 devices: a whole 2x2x4 slice. The times are simulated.
32 devices in a mesh: gx: 8 (over y, x, core), gy: 4 (over z).
Axes of the slice: x: 2, y: 2, z: 4, core: 2. Of those that a mesh axis runs over, the one named last changes fastest.
Arguments:
- right_side: float32 [32, 256, 256], P('gx', 'gy'), may hold values from -40 to 40
- kappa_sq: float32 [32, 256, 256], P('gx', 'gy'), may hold values from 0.5 to 4
Outputs:
- solution_field: float32 [32, 256, 256], P('gx', 'gy')
- residual: float32 [32, 256, 256], P('gx', 'gy')
- residual_rms: float32 [3], replicated
All inputs are finite; a program needn't handle non-finite values.
Results may differ from a plain program's by a relative error of at most 0.00016.
Values sent between devices are 32-bit elements; how exact they have to be, the bound alone decides.
A program may use at most 64 MiB of HBM per device.

v0:
```python
import jax
import jax.numpy as jnp
from jax import lax
from jax.sharding import PartitionSpec as P

ITERS = 3


def extended(x, sides, width):
    for axis, dim in sides:
        size, length = (lax.axis_size(axis), x.shape[dim])
        up = [(i, (i + 1) % size) for i in range(size)]
        down = [(j, i) for i, j in up]
        last = lax.slice_in_dim(x, length - width, length, axis=dim)
        first = lax.slice_in_dim(x, 0, width, axis=dim)
        before = lax.ppermute(last, axis, up)
        after = lax.ppermute(first, axis, down)
        x = jnp.concatenate([before, x, after], axis=dim)
    return x


def zbeside(field):
    return jnp.roll(field, 1, 2) + jnp.roll(field, -1, 2)


def operate_double(field, kappa_wide, kappa_sq):
    padded = extended(field, (("gx", 0), ("gy", 1)), 2)
    center = padded[1:-1, 1:-1]
    beside = padded[2:, 1:-1] + padded[:-2, 1:-1]
    beside = beside + padded[1:-1, 2:] + padded[1:-1, :-2]
    beside = beside + zbeside(center)
    middle = (6.0 + kappa_wide) * center - beside
    inner = middle[1:-1, 1:-1]
    outer = middle[2:, 1:-1] + middle[:-2, 1:-1]
    outer = outer + middle[1:-1, 2:] + middle[1:-1, :-2]
    outer = outer + zbeside(inner)
    return (6.0 + kappa_sq) * inner - outer


def body(right_side, kappa_sq):
    shifted = 6.0 + kappa_sq
    precond = 1.0 / (shifted * shifted + 6.0)
    cells = (
        right_side.shape[0]
        * lax.axis_size("gx")
        * right_side.shape[1]
        * lax.axis_size("gy")
        * right_side.shape[2]
    )
    kappa_wide = extended(kappa_sq, (("gx", 0), ("gy", 1)), 1)

    def operate(field):
        return operate_double(field, kappa_wide, kappa_sq)

    solution_field = jnp.zeros_like(right_side)
    residual = right_side
    u_vec = precond * residual
    w_vec = operate(u_vec)
    p_vec = jnp.zeros_like(right_side)
    s_vec = jnp.zeros_like(right_side)
    q_vec = jnp.zeros_like(right_side)
    z_vec = jnp.zeros_like(right_side)
    norms = []
    gamma_old = jnp.float32(1.0)
    alpha_old = jnp.float32(1.0)
    for step in range(ITERS):
        gamma, delta, norm_sq = lax.psum(
            (jnp.sum(residual * u_vec), jnp.sum(w_vec * u_vec), jnp.sum(residual * residual)),
            ("gx", "gy"),
        )
        norms.append(jnp.sqrt(norm_sq / cells))
        m_vec = precond * w_vec
        n_vec = operate(m_vec)
        if step == 0:
            beta = jnp.float32(0.0)
            alpha = gamma / delta
        else:
            beta = gamma / gamma_old
            alpha = gamma / (delta - beta * gamma / alpha_old)
        z_vec = n_vec + beta * z_vec
        q_vec = m_vec + beta * q_vec
        s_vec = w_vec + beta * s_vec
        p_vec = u_vec + beta * p_vec
        solution_field = solution_field + alpha * p_vec
        residual = residual - alpha * s_vec
        u_vec = u_vec - alpha * q_vec
        w_vec = w_vec - alpha * z_vec
        gamma_old = gamma
        alpha_old = alpha
    return (solution_field, residual, jnp.stack(norms))


def solution(mesh):
    return jax.shard_map(
        body,
        mesh=mesh,
        in_specs=(P("gx", "gy", None), P("gx", "gy", None)),
        out_specs=(P("gx", "gy", None), P("gx", "gy", None), P()),
        check_vma=False,
    )
```

profile of v0, /device:TPU:0, one launch (start us, length us, event | category | flops | bytes accessed | tf_op | source)
XLA Modules:
  0.0 183.8 jit_solution(11298352083403069376)
XLA Ops:
  0.6 0.9 fusion.42
  1.6 0.5 collective-permute-start
  2.1 2.9 %collective-permute-start.1 = (f32[1,64,256]{2,1,0:T(8,128)S(1)}, f32[1,64,256]{2,1,0:T(8,128)S(1)}, u32[]{:S(2)}, u32[]{:S(2)}) collective-permute-start(f32[1,64,256]{2,1,0:T(8,128)S(1)} %get-tuple-element.61), channel_id=1, source_target_pairs={{4,0},{8,4},{12,8},{16,12},{20,16},{24,20},{28,24},{0,28},{5,1},{9... | collective-permute-start | bytes 196616 | tf_op jit(solution)/shard_map/ppermute | solution.py:17
  5.0 1.9 %collective-permute-done = f32[1,64,256]{2,1,0:T(8,128)S(1)} collective-permute-done((f32[1,64,256]{2,1,0:T(8,128)S(1)}, f32[1,64,256]{2,1,0:T(8,128)S(1)}, u32[]{:S(2)}, u32[]{:S(2)}) %collective-permute-start) | collective-permute-done | bytes 65568 | tf_op jit(solution)/shard_map/ppermute | solution.py:16
  6.9 1.0 constant_dynamic-update-slice_fusion.1
  8.0 0.1 collective-permute-start.4
  8.0 2.6 %collective-permute-start.5 = (f32[2,64,256]{2,1,0:T(8,128)S(1)}, f32[2,64,256]{2,1,0:T(8,128)S(1)}, u32[]{:S(2)}, u32[]{:S(2)}) collective-permute-start(f32[2,64,256]{2,1,0:T(8,128)S(1)} %get-tuple-element.66), channel_id=1, source_target_pairs={{4,0},{8,4},{12,8},{16,12},{20,16},{24,20},{28,24},{0,28},{5,1},{9... | collective-permute-start | bytes 393224 | tf_op jit(solution)/shard_map/ppermute | solution.py:17
  10.7 0.0 collective-permute-done.1
  10.7 2.6 %collective-permute-done.4 = f32[2,64,256]{2,1,0:T(8,128)S(1)} collective-permute-done((f32[2,64,256]{2,1,0:T(8,128)S(1)}, f32[2,64,256]{2,1,0:T(8,128)S(1)}, u32[]{:S(2)}, u32[]{:S(2)}) %collective-permute-start.4) | collective-permute-done | bytes 131104 | tf_op jit(solution)/shard_map/ppermute | solution.py:16
  13.3 0.0 collective-permute-done.5
  13.3 4.9 %collective-permute-start.7 = (f32[8,2,256]{2,1,0:T(2,128)S(1)}, f32[8,2,256]{2,1,0:T(2,128)S(1)}, u32[]{:S(2)}, u32[]{:S(2)}) collective-permute-start(f32[8,2,256]{2,1,0:T(2,128)S(1)} %get-tuple-element.41), channel_id=1, source_target_pairs={{1,0},{2,1},{3,2},{0,3},{5,4},{6,5},{7,6},{4,7},{9,8},{10,9},{11,1... | collective-permute-start | bytes 49160 | tf_op jit(solution)/shard_map/ppermute | solution.py:17
  18.2 0.0 collective-permute-start.6
  18.2 0.1 collective-permute-start.2
  18.3 3.9 %collective-permute-start.3 = (f32[6,1,256]{2,1,0:T(1,128)S(1)}, f32[6,1,256]{2,1,0:T(1,128)S(1)}, u32[]{:S(2)}, u32[]{:S(2)}) collective-permute-start(f32[6,1,256]{2,1,0:T(1,128)S(1)} %get-tuple-element.56), channel_id=1, source_target_pairs={{1,0},{2,1},{3,2},{0,3},{5,4},{6,5},{7,6},{4,7},{9,8},{10,9},{11,1... | collective-permute-start | bytes 18440 | tf_op jit(solution)/shard_map/ppermute | solution.py:17
  22.2 0.0 collective-permute-done.7
  22.2 1.6 collective-permute-done.6
  23.7 0.1 pad_maximum_fusion
  23.8 0.2 fusion.31
  24.0 0.1 fusion.32
  24.1 0.0 collective-permute-done.2
  24.2 0.0 collective-permute-done.3
  24.2 0.4 fusion.10
  24.5 0.1 fusion.37
  24.6 0.0 copy-start.1
  24.6 0.1 fusion.38
  24.8 0.8 copy-done.1
  25.6 0.8 multiply_reduce_fusion.7
  26.4 0.1 fusion.22
  26.5 0.1 collective-permute-start.8
  26.6 2.6 %collective-permute-start.9 = (f32[2,64,256]{2,1,0:T(8,128)S(1)}, f32[2,64,256]{2,1,0:T(8,128)S(1)}, u32[]{:S(2)}, u32[]{:S(2)}) collective-permute-start(f32[2,64,256]{2,1,0:T(8,128)S(1)} %get-tuple-element.60), channel_id=1, source_target_pairs={{4,0},{8,4},{12,8},{16,12},{20,16},{24,20},{28,24},{0,28},{5,1},{9... | collective-permute-start | bytes 393224 | tf_op jit(solution)/shard_map/ppermute | solution.py:17
  29.2 3.9 %collective-permute-done.8 = f32[2,64,256]{2,1,0:T(8,128)S(1)} collective-permute-done((f32[2,64,256]{2,1,0:T(8,128)S(1)}, f32[2,64,256]{2,1,0:T(8,128)S(1)}, u32[]{:S(2)}, u32[]{:S(2)}) %collective-permute-start.8) | collective-permute-done | bytes 131104 | tf_op jit(solution)/shard_map/ppermute | solution.py:16
  33.1 0.0 collective-permute-done.9
  33.1 3.5 %collective-permute-start.11 = (f32[8,2,256]{2,1,0:T(2,128)S(1)}, f32[8,2,256]{2,1,0:T(2,128)S(1)}, u32[]{:S(2)}, u32[]{:S(2)}) collective-permute-start(f32[8,2,256]{2,1,0:T(2,128)S(1)} %get-tuple-element.39), channel_id=1, source_target_pairs={{1,0},{2,1},{3,2},{0,3},{5,4},{6,5},{7,6},{4,7},{9,8},{10,9},{11,1... | collective-permute-start | bytes 49160 | tf_op jit(solution)/shard_map/ppermute | solution.py:17
  36.6 0.0 collective-permute-start.10
  36.6 39.5 %all-reduce.2 = (f32[]{:T(128)}, f32[]{:T(128)}) all-reduce(f32[]{:T(128)} %get-tuple-element.11, f32[]{:T(128)} %get-tuple-element.10), channel_id=1, replica_groups=mesh['gx'=8,'gy'=4] {'gx','gy'}, use_global_device_ids=true, to_apply=%region_1.2 | all-reduce | flops 2 | bytes 16 | tf_op jit(solution)/shard_map/psum | solution.py:67
  77.4 0.0 collective-permute-done.11
  77.4 0.0 collective-permute-done.10
  77.4 0.1 pad_maximum_fusion.1
  77.5 0.1 fusion.30
  77.7 0.2 fusion.29
  77.8 0.4 fusion.6
  78.2 0.1 fusion.35
  78.3 0.1 fusion.36
  78.5 1.0 multiply_reduce_fusion.5
  79.5 0.1 fusion.21
  79.6 0.1 collective-permute-start.12
  79.6 2.6 %collective-permute-start.13 = (f32[2,64,256]{2,1,0:T(8,128)S(1)}, f32[2,64,256]{2,1,0:T(8,128)S(1)}, u32[]{:S(2)}, u32[]{:S(2)}) collective-permute-start(f32[2,64,256]{2,1,0:T(8,128)S(1)} %get-tuple-element.58), channel_id=1, source_target_pairs={{4,0},{8,4},{12,8},{16,12},{20,16},{24,20},{28,24},{0,28},{5,1},{9... | collective-permute-start | bytes 393224 | tf_op jit(solution)/shard_map/ppermute | solution.py:17
  82.3 2.6 %collective-permute-done.12 = f32[2,64,256]{2,1,0:T(8,128)S(1)} collective-permute-done((f32[2,64,256]{2,1,0:T(8,128)S(1)}, f32[2,64,256]{2,1,0:T(8,128)S(1)}, u32[]{:S(2)}, u32[]{:S(2)}) %collective-permute-start.12) | collective-permute-done | bytes 131104 | tf_op jit(solution)/shard_map/ppermute | solution.py:16
  84.9 0.3 collective-permute-done.13
  85.2 1.6 collective-permute-start.15
  86.8 0.6 collective-permute-start.14
  87.5 41.0 %all-reduce.1 = (f32[]{:T(128)}, f32[]{:T(128)}) all-reduce(f32[]{:T(128)} %get-tuple-element.6, f32[]{:T(128)} %get-tuple-element.5), channel_id=1, replica_groups=mesh['gx'=8,'gy'=4] {'gx','gy'}, use_global_device_ids=true, to_apply=%region_5.6 | all-reduce | flops 2 | bytes 16 | tf_op jit(solution)/shard_map/psum | solution.py:67
  133.1 0.0 collective-permute-done.15
  133.1 0.0 collective-permute-done.14
  133.1 0.1 pad_maximum_fusion.2
  133.1 0.1 fusion.28
  133.3 0.2 fusion.27
  133.5 0.4 fusion.2
  133.8 0.1 fusion.33
  133.9 0.1 fusion.34
  134.1 1.0 multiply_reduce_fusion
  135.1 41.3 %all-reduce = (f32[]{:T(128)}, f32[]{:T(128)}, f32[]{:T(128)}, f32[]{:T(128)}, f32[]{:T(128)}) all-reduce(f32[]{:T(128)} %get-tuple-element.4, f32[]{:T(128)} %get-tuple-element.9, f32[]{:T(128)} %get-tuple-element.3, f32[]{:T(128)} %get-tuple-element.7, f32[]{:T(128)} %get-tuple-element.8), channel_id=1, replica_groups=mesh['gx'=8,'gy'=4] {'gx','gy'}, use_global_device_ids=true, to_apply=%region_9.10 | all-reduce | flops 5 | bytes 40 | tf_op jit(solution)/shard_map/psum | solution.py:67
  182.3 1.0 multiply_subtract_fusion
  183.3 0.6 pad_maximum_fusion.30
  (11 shorter events, 0.1 us)
Async XLA Ops:
  0.6 6.3 %copy-start = (f32[4,64,256]{2,1,0:T(8,128)S(1)}, f32[4,64,256]{2,1,0:T(8,128)}, u32[]{:S(2)}) copy-start(f32[4,64,256]{2,1,0:T(8,128)} %param.3) | copy-start | bytes 786436
  1.6 5.4 %collective-permute-start = (f32[1,64,256]{2,1,0:T(8,128)S(1)}, f32[1,64,256]{2,1,0:T(8,128)S(1)}, u32[]{:S(2)}, u32[]{:S(2)}) collective-permute-start(f32[1,64,256]{2,1,0:T(8,128)S(1)} %get-tuple-element.62), channel_id=1, source_target_pairs={{0,4},{4,8},{8,12},{12,16},{16,20},{20,24},{24,28},{28,0},{1,5},{5... | collective-permute-start | bytes 196616 | tf_op jit(solution)/shard_map/ppermute | solution.py:16
  2.1 8.6 %collective-permute-start.1 = (f32[1,64,256]{2,1,0:T(8,128)S(1)}, f32[1,64,256]{2,1,0:T(8,128)S(1)}, u32[]{:S(2)}, u32[]{:S(2)}) collective-permute-start(f32[1,64,256]{2,1,0:T(8,128)S(1)} %get-tuple-element.61), channel_id=1, source_target_pairs={{4,0},{8,4},{12,8},{16,12},{20,16},{24,20},{28,24},{0,28},{5,1},{9... | collective-permute-start | bytes 196616 | tf_op jit(solution)/shard_map/ppermute | solution.py:17
  8.0 5.3 %collective-permute-start.4 = (f32[2,64,256]{2,1,0:T(8,128)S(1)}, f32[2,64,256]{2,1,0:T(8,128)S(1)}, u32[]{:S(2)}, u32[]{:S(2)}) collective-permute-start(f32[2,64,256]{2,1,0:T(8,128)S(1)} %get-tuple-element.65), channel_id=1, source_target_pairs={{0,4},{4,8},{8,12},{12,16},{16,20},{20,24},{24,28},{28,0},{1,5},{5... | collective-permute-start | bytes 393224 | tf_op jit(solution)/shard_map/ppermute | solution.py:16
  8.0 5.3 %collective-permute-start.5 = (f32[2,64,256]{2,1,0:T(8,128)S(1)}, f32[2,64,256]{2,1,0:T(8,128)S(1)}, u32[]{:S(2)}, u32[]{:S(2)}) collective-permute-start(f32[2,64,256]{2,1,0:T(8,128)S(1)} %get-tuple-element.66), channel_id=1, source_target_pairs={{4,0},{8,4},{12,8},{16,12},{20,16},{24,20},{28,24},{0,28},{5,1},{9... | collective-permute-start | bytes 393224 | tf_op jit(solution)/shard_map/ppermute | solution.py:17
  13.3 8.8 %collective-permute-start.7 = (f32[8,2,256]{2,1,0:T(2,128)S(1)}, f32[8,2,256]{2,1,0:T(2,128)S(1)}, u32[]{:S(2)}, u32[]{:S(2)}) collective-permute-start(f32[8,2,256]{2,1,0:T(2,128)S(1)} %get-tuple-element.41), channel_id=1, source_target_pairs={{1,0},{2,1},{3,2},{0,3},{5,4},{6,5},{7,6},{4,7},{9,8},{10,9},{11,1... | collective-permute-start | bytes 49160 | tf_op jit(solution)/shard_map/ppermute | solution.py:17
  18.2 5.5 %collective-permute-start.6 = (f32[8,2,256]{2,1,0:T(2,128)S(1)}, f32[8,2,256]{2,1,0:T(2,128)S(1)}, u32[]{:S(2)}, u32[]{:S(2)}) collective-permute-start(f32[8,2,256]{2,1,0:T(2,128)S(1)} %get-tuple-element.42), channel_id=1, source_target_pairs={{0,1},{1,2},{2,3},{3,0},{4,5},{5,6},{6,7},{7,4},{8,9},{9,10},{10,1... | collective-permute-start | bytes 49160 | tf_op jit(solution)/shard_map/ppermute | solution.py:16
  18.2 5.9 %collective-permute-start.2 = (f32[6,1,256]{2,1,0:T(1,128)S(1)}, f32[6,1,256]{2,1,0:T(1,128)S(1)}, u32[]{:S(2)}, u32[]{:S(2)}) collective-permute-start(f32[6,1,256]{2,1,0:T(1,128)S(1)} %get-tuple-element.55), channel_id=1, source_target_pairs={{0,1},{1,2},{2,3},{3,0},{4,5},{5,6},{6,7},{7,4},{8,9},{9,10},{10,1... | collective-permute-start | bytes 18440 | tf_op jit(solution)/shard_map/ppermute | solution.py:16
  18.3 5.9 %collective-permute-start.3 = (f32[6,1,256]{2,1,0:T(1,128)S(1)}, f32[6,1,256]{2,1,0:T(1,128)S(1)}, u32[]{:S(2)}, u32[]{:S(2)}) collective-permute-start(f32[6,1,256]{2,1,0:T(1,128)S(1)} %get-tuple-element.56), channel_id=1, source_target_pairs={{1,0},{2,1},{3,2},{0,3},{5,4},{6,5},{7,6},{4,7},{9,8},{10,9},{11,1... | collective-permute-start | bytes 18440 | tf_op jit(solution)/shard_map/ppermute | solution.py:17
  24.6 1.0 copy-start.1
  26.5 6.6 %collective-permute-start.8 = (f32[2,64,256]{2,1,0:T(8,128)S(1)}, f32[2,64,256]{2,1,0:T(8,128)S(1)}, u32[]{:S(2)}, u32[]{:S(2)}) collective-permute-start(f32[2,64,256]{2,1,0:T(8,128)S(1)} %get-tuple-element.59), channel_id=1, source_target_pairs={{0,4},{4,8},{8,12},{12,16},{16,20},{20,24},{24,28},{28,0},{1,5},{5... | collective-permute-start | bytes 393224 | tf_op jit(solution)/shard_map/ppermute | solution.py:16
  26.6 6.6 %collective-permute-start.9 = (f32[2,64,256]{2,1,0:T(8,128)S(1)}, f32[2,64,256]{2,1,0:T(8,128)S(1)}, u32[]{:S(2)}, u32[]{:S(2)}) collective-permute-start(f32[2,64,256]{2,1,0:T(8,128)S(1)} %get-tuple-element.60), channel_id=1, source_target_pairs={{4,0},{8,4},{12,8},{16,12},{20,16},{24,20},{28,24},{0,28},{5,1},{9... | collective-permute-start | bytes 393224 | tf_op jit(solution)/shard_map/ppermute | solution.py:17
  33.1 44.3 %collective-permute-start.11 = (f32[8,2,256]{2,1,0:T(2,128)S(1)}, f32[8,2,256]{2,1,0:T(2,128)S(1)}, u32[]{:S(2)}, u32[]{:S(2)}) collective-permute-start(f32[8,2,256]{2,1,0:T(2,128)S(1)} %get-tuple-element.39), channel_id=1, source_target_pairs={{1,0},{2,1},{3,2},{0,3},{5,4},{6,5},{7,6},{4,7},{9,8},{10,9},{11,1... | collective-permute-start | bytes 49160 | tf_op jit(solution)/shard_map/ppermute | solution.py:17
  36.6 40.8 %collective-permute-start.10 = (f32[8,2,256]{2,1,0:T(2,128)S(1)}, f32[8,2,256]{2,1,0:T(2,128)S(1)}, u32[]{:S(2)}, u32[]{:S(2)}) collective-permute-start(f32[8,2,256]{2,1,0:T(2,128)S(1)} %get-tuple-element.40), channel_id=1, source_target_pairs={{0,1},{1,2},{2,3},{3,0},{4,5},{5,6},{6,7},{7,4},{8,9},{9,10},{10,1... | collective-permute-start | bytes 49160 | tf_op jit(solution)/shard_map/ppermute | solution.py:16
  79.6 5.3 %collective-permute-start.12 = (f32[2,64,256]{2,1,0:T(8,128)S(1)}, f32[2,64,256]{2,1,0:T(8,128)S(1)}, u32[]{:S(2)}, u32[]{:S(2)}) collective-permute-start(f32[2,64,256]{2,1,0:T(8,128)S(1)} %get-tuple-element.57), channel_id=1, source_target_pairs={{0,4},{4,8},{8,12},{12,16},{16,20},{20,24},{24,28},{28,0},{1,5},{5... | collective-permute-start | bytes 393224 | tf_op jit(solution)/shard_map/ppermute | solution.py:16
  79.6 5.6 %collective-permute-start.13 = (f32[2,64,256]{2,1,0:T(8,128)S(1)}, f32[2,64,256]{2,1,0:T(8,128)S(1)}, u32[]{:S(2)}, u32[]{:S(2)}) collective-permute-start(f32[2,64,256]{2,1,0:T(8,128)S(1)} %get-tuple-element.58), channel_id=1, source_target_pairs={{4,0},{8,4},{12,8},{16,12},{20,16},{24,20},{28,24},{0,28},{5,1},{9... | collective-permute-start | bytes 393224 | tf_op jit(solution)/shard_map/ppermute | solution.py:17
  85.2 47.8 %collective-permute-start.15 = (f32[8,2,256]{2,1,0:T(2,128)S(1)}, f32[8,2,256]{2,1,0:T(2,128)S(1)}, u32[]{:S(2)}, u32[]{:S(2)}) collective-permute-start(f32[8,2,256]{2,1,0:T(2,128)S(1)} %get-tuple-element.37), channel_id=1, source_target_pairs={{1,0},{2,1},{3,2},{0,3},{5,4},{6,5},{7,6},{4,7},{9,8},{10,9},{11,1... | collective-permute-start | bytes 49160 | tf_op jit(solution)/shard_map/ppermute | solution.py:17
  86.8 46.3 %collective-permute-start.14 = (f32[8,2,256]{2,1,0:T(2,128)S(1)}, f32[8,2,256]{2,1,0:T(2,128)S(1)}, u32[]{:S(2)}, u32[]{:S(2)}) collective-permute-start(f32[8,2,256]{2,1,0:T(2,128)S(1)} %get-tuple-element.38), channel_id=1, source_target_pairs={{0,1},{1,2},{2,3},{3,0},{4,5},{5,6},{6,7},{7,4},{8,9},{9,10},{10,1... | collective-permute-start | bytes 49160 | tf_op jit(solution)/shard_map/ppermute | solution.py:16
where the time goes:
time: 185 us; the launch traced here: 184 us
  blocking collectives  122 us (66%)
  starting transfers between devices  26.1 us (14%)
  waiting for transfers between devices  13 us (7%)
  between operations  12.7 us (7%)
  other arithmetic  6.86 us (4%)
  local copies, waits for them, and re-layouts  3.47 us (2%)
    psum x3, blocking collectives, body(): lax.psum((jnp.sum(residual * u_vec), jnp.sum(w_vec * u_vec), jnp.sum(resi...  122 us
    ppermute x8, starting transfers between devices, extended(): after = lax.ppermute(first, axis, down)  24.6 us
    ppermute x8, waiting for transfers between devices, extended(): before = lax.ppermute(last, axis, up)  12.7 us
  transfers between devices with their start and end apart: 16, of which 6 were waited for; matrix products, arithmetic and copies ran while one was open for 1% of the time, Pallas kernels for 0%

commit v1 on v0

v1 whole, which is shorter than its diff:
```python
import functools
import jax
import jax.numpy as jnp
from jax import lax
from jax.experimental import pallas as pl
from jax.experimental.pallas import tpu as pltpu
from jax.sharding import PartitionSpec as P

ITERS = 3
MESH = pl.DeviceIdType.MESH


def shifted(c):
    return [None] + c[:-1]


def plus(a, b, scale):
    out = []
    for one, two in zip(a, b):
        two = None if two is None else two * scale
        out.append(one if two is None else two if one is None else one + two)
    return out


def form(c, entry):
    total = None
    for i, one in enumerate(c):
        for j, two in enumerate(c):
            if one is not None and two is not None and i < ITERS and j < ITERS:
                term = one * two * entry(i, j)
                total = term if total is None else total + term
    return total


def coefficients(mu, dots, cells):
    one = jnp.ones_like(mu[0])
    res = [one] + [None] * ITERS
    step = [None] * (ITERS + 1)
    sol = [None] * (ITERS + 1)
    norms = []
    for i in range(ITERS):
        gamma = form(res, lambda a, b: mu[a + b])
        delta = form(res, lambda a, b: mu[a + b + 1])
        norms.append(jnp.sqrt(form(res, lambda a, b: dots[min(a, b), max(a, b)]) / cells))
        if i == 0:
            alpha = gamma / delta
            step = list(res)
        else:
            beta = gamma / gamma_old
            alpha = gamma / (delta - beta * gamma / alpha_old)
            step = plus(res, step, beta)
        sol = plus(sol, step, alpha)
        res = plus(res, shifted(step), -alpha)
        gamma_old, alpha_old = gamma, alpha
    return sol, res, norms


def kernel(
    nx, ny, cells, rhs_hbm, kappa_hbm, sol_ref, res_ref, norms_ref,
    v_ref, y_ref, t_ref, d_ref, m_ref, face_ref, edge_out, edge_in, corner_out, corner_in,
    slots, load_sem, face_send, face_recv, edge_send, edge_recv, corner_send, corner_recv,
    sum_send, sum_recv,
):
    layers, rows, cols = rhs_hbm.shape
    ix, iy = lax.axis_index("gx"), lax.axis_index("gy")
    count = nx * ny
    me = ix * ny + iy
    load_k = pltpu.make_async_copy(kappa_hbm, d_ref, load_sem.at[0])
    load_r = pltpu.make_async_copy(rhs_hbm, v_ref.at[0], load_sem.at[1])
    load_k.start()
    load_r.start()

    barrier = pltpu.get_barrier_semaphore()

    def greet(k, carry):
        other = lax.rem(me + k, count)
        pl.semaphore_signal(
            barrier, inc=1, device_id=(other // ny, lax.rem(other, ny)), device_id_type=MESH
        )
        return carry

    lax.fori_loop(1, count, greet, 0)

    x_of = (lax.rem(ix + nx - 1, nx), lax.rem(ix + 1, nx))
    y_of = (lax.rem(iy + ny - 1, ny), lax.rem(iy + 1, ny))
    row = lax.broadcasted_iota(jnp.int32, (rows, cols), 0)
    first, last = row == 0, row == rows - 1

    def lateral(x):
        up = jnp.where(first, 0.0, pltpu.roll(x, 1, 0))
        down = jnp.where(last, 0.0, pltpu.roll(x, rows - 1, 0))
        return (pltpu.roll(x, 1, 1) + pltpu.roll(x, cols - 1, 1)) + (up + down)

    def local_k(get, l):
        x = get(l)
        out = d_ref[l] * x - lateral(x)
        if l > 0:
            out = out - get(l - 1)
        if l < layers - 1:
            out = out - get(l + 1)
        return out

    def tile_sum(x):
        return jnp.sum(x, axis=(0, 1), keepdims=True)

    load_k.wait()
    for l in range(layers):
        d = 6.0 + d_ref[l]
        d_ref[l] = d
        m_ref[l] = 1.0 / (d * d + 6.0)
    load_r.wait()

    ends = (0, layers - 1)
    mu, dots = ([], {})
    for j in range(ITERS):
        order = [0, layers - 1] + list(range(1, layers - 1)) if layers > 1 else [0]
        for l in order:
            y_ref[j, l] = m_ref[l] * v_ref[j, l]
        for side in range(2):
            at = (0, rows - 1)[side]
            for k in range(2):
                corner_out[j, 2 * k + side] = y_ref[j, ends[k], pl.ds(at, 1), :]
        if j == 0:
            pl.semaphore_wait(barrier, count - 1)
        copies = []
        for k in range(2):
            copies.append(
                pltpu.make_async_remote_copy(
                    src_ref=y_ref.at[j, ends[k]],
                    dst_ref=face_ref.at[j, 1 - k, 0],
                    send_sem=face_send.at[j, 1 - k, 0],
                    recv_sem=face_recv.at[j, 1 - k, 0],
                    device_id=(x_of[k], iy),
                    device_id_type=MESH,
                )
            )
        for k in range(2):
            for side in range(2):
                copies.append(
                    pltpu.make_async_remote_copy(
                        src_ref=corner_out.at[j, 2 * k + side],
                        dst_ref=corner_in.at[j, 2 * (1 - k) + 1 - side],
                        send_sem=corner_send.at[j, 2 * (1 - k) + 1 - side],
                        recv_sem=corner_recv.at[j, 2 * (1 - k) + 1 - side],
                        device_id=(x_of[k], y_of[side]),
                        device_id_type=MESH,
                    )
                )
        for copy in copies:
            copy.start()
        get_y = lambda l: y_ref[j, l]
        for l in order:
            t_ref[j, l] = local_k(get_y, l)
        for side in range(2):
            at = (0, rows - 1)[side]
            for l in range(layers):
                edge_out[j, side, pl.ds(l, 1), :] = y_ref[j, l, pl.ds(at, 1), :]
                edge_out[j, side, pl.ds(layers + l, 1), :] = t_ref[j, l, pl.ds(at, 1), :]
        later = []
        for side in range(2):
            later.append(
                pltpu.make_async_remote_copy(
                    src_ref=edge_out.at[j, side],
                    dst_ref=edge_in.at[j, 1 - side],
                    send_sem=edge_send.at[j, 1 - side],
                    recv_sem=edge_recv.at[j, 1 - side],
                    device_id=(ix, y_of[side]),
                    device_id_type=MESH,
                )
            )
        for k in range(2):
            later.append(
                pltpu.make_async_remote_copy(
                    src_ref=t_ref.at[j, ends[k]],
                    dst_ref=face_ref.at[j, 1 - k, 1],
                    send_sem=face_send.at[j, 1 - k, 1],
                    recv_sem=face_recv.at[j, 1 - k, 1],
                    device_id=(x_of[k], iy),
                    device_id_type=MESH,
                )
            )
        for copy in later:
            copy.start()
        copies = copies + later
        mu.append(tile_sum(sum(v_ref[j, l] * y_ref[j, l] for l in range(layers))))
        for i in range(j + 1):
            dots[i, j] = tile_sum(sum(v_ref[i, l] * v_ref[j, l] for l in range(layers)))
        for copy in copies:
            copy.wait()
        full = ITERS + j % 2
        for k in range(2):
            face_ref[j, k, 1] = face_ref[j, k, 1] - y_ref[j, ends[k]]
        for l in range(layers):
            t = t_ref[j, l]
            if l == 0:
                t = t - face_ref[j, 0, 0]
            if l == layers - 1:
                t = t - face_ref[j, 1, 0]
            t_ref[full, l] = t
            for side in range(2):
                at = pl.ds((0, rows - 1)[side], 1)
                t_ref[full, l, at, :] = t_ref[full, l, at, :] - edge_in[j, side, pl.ds(l, 1), :]
        mu.append(tile_sum(sum(t_ref[full, l] * t_ref[full, l] for l in range(layers))))
        if j == ITERS - 1:
            start_sums(mu, dots, slots, sum_send, sum_recv, me, count, ny)
        get_t = lambda l: t_ref[full, l]
        for l in range(layers):
            v = local_k(get_t, l)
            if l == 0:
                v = v - face_ref[j, 0, 1]
            if l == layers - 1:
                v = v - face_ref[j, 1, 1]
            v_ref[j + 1, l] = v
            for side in range(2):
                at = pl.ds((0, rows - 1)[side], 1)
                line = v_ref[j + 1, l, at, :] + y_ref[j, l, at, :]
                line = line - edge_in[j, side, pl.ds(layers + l, 1), :]
                for k in range(2):
                    if l == ends[k]:
                        line = line + 2.0 * corner_in[j, 2 * k + side]
                v_ref[j + 1, l, at, :] = line

    all_slots = slots.at[pl.ds(0, count - 1)]
    pltpu.make_async_copy(all_slots, all_slots, sum_send).wait()
    pltpu.make_async_copy(all_slots, all_slots, sum_recv).wait()
    total = jnp.sum(slots[...], axis=0)
    names = [("mu", i) for i in range(2 * ITERS)] + sorted(dots)
    got = {name: total[:, k : k + 1] for k, name in enumerate(names)}
    mu = [got["mu", i] for i in range(2 * ITERS)]
    sol, res, norms = coefficients(mu, got, float(cells))
    for i in range(ITERS):
        norms_ref[i] = norms[i][0, 0]
    for l in range(layers):
        x = sol[0] * y_ref[0, l]
        r = v_ref[0, l]
        for i in range(1, ITERS):
            x = x + sol[i] * y_ref[i, l]
        for i in range(1, ITERS + 1):
            r = r + res[i] * v_ref[i, l]
        sol_ref[l] = x
        res_ref[l] = r


def start_sums(mu, dots, slots, sum_send, sum_recv, me, count, ny):
    lane = lax.broadcasted_iota(jnp.int32, (1, slots.shape[-1]), 1)
    line = jnp.zeros(lane.shape, jnp.float32)
    for k, value in enumerate(mu + [dots[name] for name in sorted(dots)]):
        line = jnp.where(lane == k, value, line)
    slots[me] = line

    def send(k, carry):
        other = lax.rem(me + k, count)
        pltpu.make_async_remote_copy(
            src_ref=slots.at[me],
            dst_ref=slots.at[me],
            send_sem=sum_send,
            recv_sem=sum_recv,
            device_id=(other // ny, lax.rem(other, ny)),
            device_id_type=MESH,
        ).start()
        return carry

    lax.fori_loop(1, count, send, 0)


def body(right_side, kappa_sq):
    nx, ny = lax.axis_size("gx"), lax.axis_size("gy")
    shape = right_side.shape
    layers, rows, cols = shape
    cells = nx * layers * ny * rows * cols
    f32 = jnp.float32
    dma = pltpu.SemaphoreType.DMA
    vmem = pl.BlockSpec(memory_space=pltpu.VMEM)
    return pl.pallas_call(
        functools.partial(kernel, nx, ny, cells),
        out_shape=(
            jax.ShapeDtypeStruct(shape, f32),
            jax.ShapeDtypeStruct(shape, f32),
            jax.ShapeDtypeStruct((ITERS,), f32),
        ),
        in_specs=[pl.BlockSpec(memory_space=pl.ANY)] * 2,
        out_specs=(vmem, vmem, pl.BlockSpec(memory_space=pltpu.SMEM)),
        scratch_shapes=[
            pltpu.VMEM((ITERS + 1,) + shape, f32),
            pltpu.VMEM((ITERS,) + shape, f32),
            pltpu.VMEM((ITERS + 2,) + shape, f32),
            pltpu.VMEM(shape, f32),
            pltpu.VMEM(shape, f32),
            pltpu.VMEM((ITERS, 2, 2, rows, cols), f32),
            pltpu.VMEM((ITERS, 2, 2 * layers, cols), f32),
            pltpu.VMEM((ITERS, 2, 2 * layers, cols), f32),
            pltpu.VMEM((ITERS, 4, 1, cols), f32),
            pltpu.VMEM((ITERS, 4, 1, cols), f32),
            pltpu.VMEM((nx * ny, 1, 128), f32),
            dma((2,)),
            dma((ITERS, 2, 2)),
            dma((ITERS, 2, 2)),
            dma((ITERS, 2)),
            dma((ITERS, 2)),
            dma((ITERS, 4)),
            dma((ITERS, 4)),
            dma(()),
            dma(()),
        ],
        compiler_params=pltpu.CompilerParams(collective_id=0, has_side_effects=True),
    )(right_side, kappa_sq)


def solution(mesh):
    return jax.shard_map(
        body,
        mesh=mesh,
        in_specs=(P("gx", "gy", None), P("gx", "gy", None)),
        out_specs=(P("gx", "gy", None), P("gx", "gy", None), P()),
        check_vma=False,
    )
```

time: 185 us -> 31.8 us (0.17)
  blocking collectives: 122 us -> 0 us
  Pallas kernels: 0 us -> 28 us
  starting transfers between devices: 26.1 us -> 0 us
  waiting for transfers between devices: 13 us -> 0 us
  between operations: 12.7 us -> 0.65 us
  other arithmetic: 6.86 us -> 0 us
    psum x3 -> x0, blocking collectives: 122 us -> none  [body(): lax.psum((jnp.sum(residual * u_vec), jnp.sum(w_vec * u_vec), jnp.sum(resi...]
    pallas_call x0 -> x1, Pallas kernels: none -> 28 us  [body(): pl.pallas_call(functools.partial(kernel, nx, ny, cells), out_shape=(jax.S...]
    ppermute x16 -> x0, starting transfers between devices: 26.1 us -> none  [the longest x8 24.6 us: extended(): after = lax.ppermute(first, axis, down)]
    ppermute x16 -> x0, waiting for transfers between devices: 13 us -> none  [the longest x8 12.7 us: extended(): before = lax.ppermute(last, axis, up)]
    reduce_sum x3 -> x0, other arithmetic: 2.83 us -> none  [the longest x2 1.82 us: body(): jnp.sum(w_vec * u_vec)]
    slice x17 -> x0, local copies, waits for them, and re-layouts: 2.65 us -> none  [the longest x12 1.66 us: zbeside(): return jnp.roll(field, 1, 2) + jnp.roll(field, -1, 2)]
    unnamed x5 -> x7, local copies, waits for them, and re-layouts: 0.81 us -> 2.94 us
    sub x4 -> x0, other arithmetic: 2.08 us -> none  [the longest x3 1.09 us: operate_double(): middle = (6.0 + kappa_wide) * center - beside]
  transfers between devices with their start and end apart: 16 -> 0, of which waited for: 6 -> 0; matrix products, arithmetic and copies ran while one was open for 1% -> 0% of each run, Pallas kernels for 0% -> 0%
where the time goes in v1:
time: 31.8 us; the launch traced here: 31.6 us
  Pallas kernels  28 us (88%)
  local copies, waits for them, and re-layouts  2.94 us (9%)
  between operations  0.65 us (2%)
    pallas_call x1, Pallas kernels, body(): pl.pallas_call(functools.partial(kernel, nx, ny, cells), out_shape=(jax.S...  28 us
    unnamed x7, local copies, waits for them, and re-layouts  2.94 us

profile of v1, /device:TPU:0, one launch (start us, length us, event | category | flops | bytes accessed | tf_op | source)
XLA Modules:
  0.0 31.6 jit_solution(10385969022145112309)
XLA Ops:
  0.6 28.0 %shard_map.49 = (f32[4,64,256]{2,1,0:T(8,128)}, f32[4,64,256]{2,1,0:T(8,128)}, f32[3]{0:T(128)}) custom-call(f32[4,64,256]{2,1,0:T(8,128)} %rhs_hbm.1, f32[4,64,256]{2,1,0:T(8,128)} %kappa_hbm.1), custom_call_target="tpu_custom_call" | custom-call | tf_op jit(solution)/shard_map/pallas_call | solution.py:274
  28.7 0.0 copy-start
  28.7 1.7 %copy.8 = f32[4,64,256]{2,1,0:T(8,128)} copy(f32[4,64,256]{2,1,0:T(8,128)} %get-tuple-element.6) | data formatting | bytes 524288
  30.4 0.0 copy-done
  30.4 0.0 copy-start.1
  30.4 0.7 %copy.9 = f32[4,64,256]{2,1,0:T(8,128)} copy(f32[4,64,256]{2,1,0:T(8,128)S(1)} %copy-done) | data formatting | bytes 524288
  31.1 0.0 copy-done.1
  31.1 0.5 %copy.10 = f32[3]{0:T(128)} copy(f32[3]{0:T(128)S(1)} %copy-done.1) | data formatting | bytes 24
Async XLA Ops:
  28.7 1.7 %copy-start = (f32[4,64,256]{2,1,0:T(8,128)S(1)}, f32[4,64,256]{2,1,0:T(8,128)}, u32[]{:S(2)}) copy-start(f32[4,64,256]{2,1,0:T(8,128)} %get-tuple-element.7) | copy-start | bytes 786436
  30.4 0.7 %copy-start.1 = (f32[3]{0:T(128)S(1)}, f32[3]{0:T(128)}, u32[]{:S(2)}) copy-start(f32[3]{0:T(128)} %get-tuple-element.8) | copy-start | bytes 40

commit v2 on v1

v2 whole, which is shorter than its diff:
```python
import functools
import jax
import jax.numpy as jnp
from jax import lax
from jax.experimental import pallas as pl
from jax.experimental.pallas import tpu as pltpu
from jax.sharding import PartitionSpec as P

ITERS = 3
MESH = pl.DeviceIdType.MESH


def shifted(c):
    return [None] + c[:-1]


def plus(a, b, scale):
    out = []
    for one, two in zip(a, b):
        two = None if two is None else two * scale
        out.append(one if two is None else two if one is None else one + two)
    return out


def form(c, entry):
    total = None
    for i, one in enumerate(c):
        for j, two in enumerate(c):
            if one is not None and two is not None and i < ITERS and j < ITERS:
                term = one * two * entry(i, j)
                total = term if total is None else total + term
    return total


def coefficients(mu, dots, cells):
    one = jnp.ones_like(mu[0])
    res = [one] + [None] * ITERS
    step = [None] * (ITERS + 1)
    sol = [None] * (ITERS + 1)
    norms = []
    for i in range(ITERS):
        gamma = form(res, lambda a, b: mu[a + b])
        delta = form(res, lambda a, b: mu[a + b + 1])
        norms.append(jnp.sqrt(form(res, lambda a, b: dots[min(a, b), max(a, b)]) / cells))
        if i == 0:
            alpha = gamma / delta
            step = list(res)
        else:
            beta = gamma / gamma_old
            alpha = gamma / (delta - beta * gamma / alpha_old)
            step = plus(res, step, beta)
        sol = plus(sol, step, alpha)
        res = plus(res, shifted(step), -alpha)
        gamma_old, alpha_old = gamma, alpha
    return sol, res, norms


def kernel(
    nx, ny, cells, rhs_hbm, kappa_hbm, *refs,
):
    (
    v_ref, y_ref, coef_ref, t_ref, d_ref, m_ref, face_ref, edge_out, edge_in, corner_out, corner_in,
    slots, load_sem, face_send, face_recv, edge_send, edge_recv, corner_send, corner_recv,
    sum_send, sum_recv,
    ) = refs
    layers, rows, cols = rhs_hbm.shape
    ix, iy = lax.axis_index("gx"), lax.axis_index("gy")
    count = nx * ny
    me = ix * ny + iy
    load_k = pltpu.make_async_copy(kappa_hbm, d_ref, load_sem.at[0])
    load_r = pltpu.make_async_copy(rhs_hbm, v_ref.at[0], load_sem.at[1])
    load_k.start()
    load_r.start()

    barrier = pltpu.get_barrier_semaphore()

    def greet(k, carry):
        other = lax.rem(me + k, count)
        pl.semaphore_signal(
            barrier, inc=1, device_id=(other // ny, lax.rem(other, ny)), device_id_type=MESH
        )
        return carry

    lax.fori_loop(1, count, greet, 0)

    x_of = (lax.rem(ix + nx - 1, nx), lax.rem(ix + 1, nx))
    y_of = (lax.rem(iy + ny - 1, ny), lax.rem(iy + 1, ny))
    row = lax.broadcasted_iota(jnp.int32, (rows, cols), 0)
    first, last = row == 0, row == rows - 1

    def lateral(x):
        up = jnp.where(first, 0.0, pltpu.roll(x, 1, 0))
        down = jnp.where(last, 0.0, pltpu.roll(x, rows - 1, 0))
        return (pltpu.roll(x, 1, 1) + pltpu.roll(x, cols - 1, 1)) + (up + down)

    def local_k(get, l):
        x = get(l)
        out = d_ref[l] * x - lateral(x)
        if l > 0:
            out = out - get(l - 1)
        if l < layers - 1:
            out = out - get(l + 1)
        return out

    def tile_sum(x):
        return jnp.sum(x, axis=(0, 1), keepdims=True)

    load_k.wait()
    for l in range(layers):
        d = 6.0 + d_ref[l]
        d_ref[l] = d
        m_ref[l] = 1.0 / (d * d + 6.0)
    load_r.wait()

    ends = (0, layers - 1)
    mu, dots = ([], {})
    sends = []
    order = [0, layers - 1] + list(range(1, layers - 1)) if layers > 1 else [0]
    inner_first = list(range(1, layers - 1)) + [0, layers - 1] if layers > 1 else [0]

    def remote(src, dst, send, recv, device):
        copy = pltpu.make_async_remote_copy(
            src_ref=src, dst_ref=dst, send_sem=send, recv_sem=recv,
            device_id=device, device_id_type=MESH,
        )
        sends.append(copy)
        return copy

    for j in range(ITERS):
        for l in order:
            y_ref[j, l] = m_ref[l] * v_ref[j, l]
        for side in range(2):
            at = pl.ds((0, rows - 1)[side], 1)
            for k in range(2):
                corner_out[j, 2 * k + side] = y_ref[j, ends[k], at, :]
            for l in range(layers):
                edge_out[j, 0, side, pl.ds(l, 1), :] = y_ref[j, l, at, :]
        if j == 0:
            pl.semaphore_wait(barrier, count - 1)
        edges = [
            [
                remote(
                    edge_out.at[j, part, side], edge_in.at[j, part, 1 - side],
                    edge_send.at[j, part, side], edge_recv.at[j, part, 1 - side],
                    (ix, y_of[side]),
                )
                for side in range(2)
            ]
            for part in range(2)
        ]
        corners = [
            remote(
                corner_out.at[j, 2 * k + side], corner_in.at[j, 2 * (1 - k) + 1 - side],
                corner_send.at[j, 2 * k + side], corner_recv.at[j, 2 * (1 - k) + 1 - side],
                (x_of[k], y_of[side]),
            )
            for k in range(2)
            for side in range(2)
        ]
        faces = [
            [
                remote(
                    src.at[j, ends[k]], face_ref.at[j, 1 - k, part],
                    face_send.at[j, k, part], face_recv.at[j, 1 - k, part],
                    (x_of[k], iy),
                )
                for k in range(2)
            ]
            for part, src in enumerate((y_ref, t_ref))
        ]
        for copy in edges[0] + corners + faces[0]:
            copy.start()
        get_y = lambda l: y_ref[j, l]
        for l in order:
            t_ref[j, l] = local_k(get_y, l)
        for side in range(2):
            for l in range(layers):
                at = pl.ds((0, rows - 1)[side], 1)
                edge_out[j, 1, side, pl.ds(l, 1), :] = t_ref[j, l, at, :]
        for copy in edges[1] + faces[1]:
            copy.start()
        mu.append(tile_sum(sum(v_ref[j, l] * y_ref[j, l] for l in range(layers))))
        for i in range(j + 1):
            dots[i, j] = tile_sum(sum(v_ref[i, l] * v_ref[j, l] for l in range(layers)))
        for copy in faces[0] + edges[0]:
            copy.wait_recv()
        full = ITERS + j % 2
        for l in range(layers):
            t = t_ref[j, l]
            if l == 0:
                t = t - face_ref[j, 0, 0]
            if l == layers - 1:
                t = t - face_ref[j, 1, 0]
            t_ref[full, l] = t
            for side in range(2):
                at = pl.ds((0, rows - 1)[side], 1)
                t_ref[full, l, at, :] = t_ref[full, l, at, :] - edge_in[j, 0, side, pl.ds(l, 1), :]
        mu.append(tile_sum(sum(t_ref[full, l] * t_ref[full, l] for l in range(layers))))
        if j == ITERS - 1:
            start_sums(mu, dots, slots, sum_send, sum_recv, me, count, ny)
        get_t = lambda l: t_ref[full, l]
        for l in range(layers):
            v = local_k(get_t, l)
            for k in range(2):
                if l == ends[k]:
                    v = v + y_ref[j, l]
            v_ref[j + 1, l] = v
            for side in range(2):
                at = pl.ds((0, rows - 1)[side], 1)
                v_ref[j + 1, l, at, :] = v_ref[j + 1, l, at, :] + y_ref[j, l, at, :]
        for copy in edges[1] + corners:
            copy.wait_recv()
        for l in range(layers):
            for side in range(2):
                at = pl.ds((0, rows - 1)[side], 1)
                line = v_ref[j + 1, l, at, :] - edge_in[j, 1, side, pl.ds(l, 1), :]
                for k in range(2):
                    if l == ends[k]:
                        line = line + 2.0 * corner_in[j, 2 * k + side]
                v_ref[j + 1, l, at, :] = line
        for copy in faces[1]:
            copy.wait_recv()
        for k in range(2):
            v_ref[j + 1, ends[k]] = v_ref[j + 1, ends[k]] - face_ref[j, k, 1]

    for copy in sends:
        copy.wait_send()
    all_slots = slots.at[pl.ds(0, count - 1)]
    pltpu.make_async_copy(all_slots, all_slots, sum_send).wait()
    pltpu.make_async_copy(all_slots, all_slots, sum_recv).wait()
    total = jnp.sum(slots[...], axis=0)
    names = [("mu", i) for i in range(2 * ITERS)] + sorted(dots)
    got = {name: total[:, k : k + 1] for k, name in enumerate(names)}
    mu = [got["mu", i] for i in range(2 * ITERS)]
    sol, res, norms = coefficients(mu, got, float(cells))
    for k, value in enumerate(norms + sol[:ITERS] + res[1:]):
        coef_ref[k] = value[0, 0]


def start_sums(mu, dots, slots, sum_send, sum_recv, me, count, ny):
    lane = lax.broadcasted_iota(jnp.int32, (1, slots.shape[-1]), 1)
    line = jnp.zeros(lane.shape, jnp.float32)
    for k, value in enumerate(mu + [dots[name] for name in sorted(dots)]):
        line = jnp.where(lane == k, value, line)
    slots[me] = line

    def send(k, carry):
        other = lax.rem(me + k, count)
        pltpu.make_async_remote_copy(
            src_ref=slots.at[me],
            dst_ref=slots.at[me],
            send_sem=sum_send,
            recv_sem=sum_recv,
            device_id=(other // ny, lax.rem(other, ny)),
            device_id_type=MESH,
        ).start()
        return carry

    lax.fori_loop(1, count, send, 0)


def finish(coef, v_ref, y_ref, sol_ref, res_ref, norms_ref):
    for i in range(ITERS):
        norms_ref[i] = coef[i]
    for l in range(v_ref.shape[1]):
        sol = coef[ITERS] * y_ref[0, l]
        res = v_ref[0, l]
        for i in range(1, ITERS):
            sol = sol + coef[ITERS + i] * y_ref[i, l]
        for i in range(1, ITERS + 1):
            res = res + coef[2 * ITERS + i - 1] * v_ref[i, l]
        sol_ref[l] = sol
        res_ref[l] = res


def body(right_side, kappa_sq):
    nx, ny = lax.axis_size("gx"), lax.axis_size("gy")
    shape = right_side.shape
    layers, rows, cols = shape
    cells = nx * layers * ny * rows * cols
    f32 = jnp.float32
    dma = pltpu.SemaphoreType.DMA
    whole = pl.BlockSpec(memory_space=pltpu.VMEM)
    smem = pl.BlockSpec(memory_space=pltpu.SMEM)
    out = pl.pallas_call(
        functools.partial(kernel, nx, ny, cells),
        out_shape=(
            pltpu.VMEM((ITERS + 1,) + shape, f32),
            pltpu.VMEM((ITERS,) + shape, f32),
            pltpu.SMEM((3 * ITERS,), f32),
        ),
        in_specs=[pl.BlockSpec(memory_space=pl.ANY)] * 2,
        out_specs=(whole, whole, smem),
        scratch_shapes=[
            pltpu.VMEM((ITERS + 2,) + shape, f32),
            pltpu.VMEM(shape, f32),
            pltpu.VMEM(shape, f32),
            pltpu.VMEM((ITERS, 2, 2, rows, cols), f32),
            pltpu.VMEM((ITERS, 2, 2, layers, cols), f32),
            pltpu.VMEM((ITERS, 2, 2, layers, cols), f32),
            pltpu.VMEM((ITERS, 4, 1, cols), f32),
            pltpu.VMEM((ITERS, 4, 1, cols), f32),
            pltpu.VMEM((nx * ny, 1, 128), f32),
            dma((2,)),
            dma((ITERS, 2, 2)),
            dma((ITERS, 2, 2)),
            dma((ITERS, 2, 2)),
            dma((ITERS, 2, 2)),
            dma((ITERS, 4)),
            dma((ITERS, 4)),
            dma(()),
            dma(()),
        ],
        compiler_params=pltpu.CompilerParams(collective_id=0, has_side_effects=True),
    )(right_side, kappa_sq)
    return pl.pallas_call(
        finish,
        out_shape=(
            jax.ShapeDtypeStruct(shape, f32),
            jax.ShapeDtypeStruct(shape, f32),
            jax.ShapeDtypeStruct((ITERS,), f32),
        ),
        in_specs=[smem, whole, whole],
        out_specs=(whole, whole, smem),
    )(out[2], *(pltpu.with_memory_space_constraint(x, pltpu.VMEM) for x in out[:2]))


def solution(mesh):
    return jax.shard_map(
        body,
        mesh=mesh,
        in_specs=(P("gx", "gy", None), P("gx", "gy", None)),
        out_specs=(P("gx", "gy", None), P("gx", "gy", None), P()),
        check_vma=False,
    )
```

time: 31.8 us -> 28.1 us (0.88)
  local copies, waits for them, and re-layouts: 2.94 us -> 0 us
  Pallas kernels: 28 us -> 27.3 us
    unnamed x7 -> x0, local copies, waits for them, and re-layouts: 2.94 us -> none
    pallas_call x1 -> x2, Pallas kernels: 28 us -> 27.3 us  [the longest x1 26.4 us: body(): pl.pallas_call(functools.partial(kernel, nx, ny, cells), out_shape=(pltpu...]
where the time goes in v2:
time: 28.1 us; the launch traced here: 28 us
  Pallas kernels  27.3 us (97%)
  between operations  0.64 us (2%)
    pallas_call x1, Pallas kernels, body(): pl.pallas_call(functools.partial(kernel, nx, ny, cells), out_shape=(pltpu...  26.4 us
    pallas_call x1, Pallas kernels, body(): pl.pallas_call(finish, out_shape=(jax.ShapeDtypeStruct(shape, f32), jax.S...  0.89 us

profile of v2, /device:TPU:0, one launch (start us, length us, event | category | flops | bytes accessed | tf_op | source)
XLA Modules:
  0.0 28.0 jit_solution(10739794380313672304)
XLA Ops:
  0.6 26.4 %shard_map.49 = (f32[4,4,64,256]{3,2,1,0:T(8,128)S(1)}, f32[3,4,64,256]{3,2,1,0:T(8,128)S(1)}, f32[9]{0:T(128)S(4)}) custom-call(f32[4,64,256]{2,1,0:T(8,128)} %rhs_hbm.1, f32[4,64,256]{2,1,0:T(8,128)} %kappa_hbm.1), custom_call_target="tpu_custom_call" | custom-call | tf_op jit(solution)/shard_map/pallas_call | solution.py:285
  27.1 0.9 %shard_map.50 = (f32[4,64,256]{2,1,0:T(8,128)}, f32[4,64,256]{2,1,0:T(8,128)}, f32[3]{0:T(128)}) custom-call(f32[9]{0:T(128)S(4)} %get-tuple-element.6.coef, f32[4,4,64,256]{3,2,1,0:T(8,128)S(1)} %get-tuple-element.7.v_ref, f32[3,4,64,256]{3,2,1,0:T(8,128)S(1)} %get-tuple-element.8.y_ref), custom_call_target="tpu_custom_call" | custom-call | tf_op jit(solution)/shard_map/pallas_call | solution.py:316

commit v3 on v2

--- a/solution.py
+++ b/solution.py
@@ -74,14 +74,31 @@
 
     barrier = pltpu.get_barrier_semaphore()
 
-    def greet(k, carry):
+    near = ny // 2 <= ITERS
+
+    def greet(x, y):
+        pl.semaphore_signal(barrier, inc=1, device_id=(x, y), device_id_type=MESH)
+
+    def greet_any(k, carry):
         other = lax.rem(me + k, count)
-        pl.semaphore_signal(
-            barrier, inc=1, device_id=(other // ny, lax.rem(other, ny)), device_id_type=MESH
-        )
+        greet(other // ny, lax.rem(other, ny))
         return carry
 
-    lax.fori_loop(1, count, greet, 0)
+    def greet_x(k, carry):
+        greet(lax.rem(ix + k, nx), iy)
+        return carry
+
+    def greet_y(k, carry):
+        greet(ix, lax.rem(iy + k, ny))
+        return carry
+
+    if near:
+        lax.fori_loop(1, ny, greet_y, 0)
+        lax.fori_loop(1, nx, greet_x, 0)
+        greetings = nx - 1 + ny - 1
+    else:
+        lax.fori_loop(1, count, greet_any, 0)
+        greetings = count - 1
 
     x_of = (lax.rem(ix + nx - 1, nx), lax.rem(ix + 1, nx))
     y_of = (lax.rem(iy + ny - 1, ny), lax.rem(iy + 1, ny))
@@ -134,9 +151,9 @@
             for k in range(2):
                 corner_out[j, 2 * k + side] = y_ref[j, ends[k], at, :]
             for l in range(layers):
-                edge_out[j, 0, side, pl.ds(l, 1), :] = y_ref[j, l, at, :]
+                edge_out[j, 0, side, l] = y_ref[j, l, at, :]
         if j == 0:
-            pl.semaphore_wait(barrier, count - 1)
+            pl.semaphore_wait(barrier, greetings)
         edges = [
             [
                 remote(
@@ -148,11 +165,14 @@
             ]
             for part in range(2)
         ]
+        relayed = near and j == 0
         corners = [
             remote(
-                corner_out.at[j, 2 * k + side], corner_in.at[j, 2 * (1 - k) + 1 - side],
-                corner_send.at[j, 2 * k + side], corner_recv.at[j, 2 * (1 - k) + 1 - side],
-                (x_of[k], y_of[side]),
+                edge_in.at[j, 0, side, ends[k]] if relayed else corner_out.at[j, 2 * k + side],
+                corner_in.at[j, 2 * (1 - k) + (side if relayed else 1 - side)],
+                corner_send.at[j, 2 * k + side],
+                corner_recv.at[j, 2 * (1 - k) + (side if relayed else 1 - side)],
+                (x_of[k], iy if relayed else y_of[side]),
             )
             for k in range(2)
             for side in range(2)
@@ -168,7 +188,7 @@
             ]
             for part, src in enumerate((y_ref, t_ref))
         ]
-        for copy in edges[0] + corners + faces[0]:
+        for copy in edges[0] + ([] if relayed else corners) + faces[0]:
             copy.start()
         get_y = lambda l: y_ref[j, l]
         for l in order:
@@ -176,13 +196,18 @@
         for side in range(2):
             for l in range(layers):
                 at = pl.ds((0, rows - 1)[side], 1)
-                edge_out[j, 1, side, pl.ds(l, 1), :] = t_ref[j, l, at, :]
+                edge_out[j, 1, side, l] = t_ref[j, l, at, :]
         for copy in edges[1] + faces[1]:
             copy.start()
         mu.append(tile_sum(sum(v_ref[j, l] * y_ref[j, l] for l in range(layers))))
         for i in range(j + 1):
             dots[i, j] = tile_sum(sum(v_ref[i, l] * v_ref[j, l] for l in range(layers)))
-        for copy in faces[0] + edges[0]:
+        for copy in edges[0]:
+            copy.wait_recv()
+        if relayed:
+            for copy in corners:
+                copy.start()
+        for copy in faces[0]:
             copy.wait_recv()
         full = ITERS + j % 2
         for l in range(layers):
@@ -194,7 +219,7 @@
             t_ref[full, l] = t
             for side in range(2):
                 at = pl.ds((0, rows - 1)[side], 1)
-                t_ref[full, l, at, :] = t_ref[full, l, at, :] - edge_in[j, 0, side, pl.ds(l, 1), :]
+                t_ref[full, l, at, :] = t_ref[full, l, at, :] - edge_in[j, 0, side, l]
         mu.append(tile_sum(sum(t_ref[full, l] * t_ref[full, l] for l in range(layers))))
         if j == ITERS - 1:
             start_sums(mu, dots, slots, sum_send, sum_recv, me, count, ny)
@@ -213,7 +238,7 @@
         for l in range(layers):
             for side in range(2):
                 at = pl.ds((0, rows - 1)[side], 1)
-                line = v_ref[j + 1, l, at, :] - edge_in[j, 1, side, pl.ds(l, 1), :]
+                line = v_ref[j + 1, l, at, :] - edge_in[j, 1, side, l]
                 for k in range(2):
                     if l == ends[k]:
                         line = line + 2.0 * corner_in[j, 2 * k + side]
@@ -296,8 +321,8 @@
             pltpu.VMEM(shape, f32),
             pltpu.VMEM(shape, f32),
             pltpu.VMEM((ITERS, 2, 2, rows, cols), f32),
-            pltpu.VMEM((ITERS, 2, 2, layers, cols), f32),
-            pltpu.VMEM((ITERS, 2, 2, layers, cols), f32),
+            pltpu.VMEM((ITERS, 2, 2, layers, 1, cols), f32),
+            pltpu.VMEM((ITERS, 2, 2, layers, 1, cols), f32),
             pltpu.VMEM((ITERS, 4, 1, cols), f32),
             pltpu.VMEM((ITERS, 4, 1, cols), f32),
             pltpu.VMEM((nx * ny, 1, 128), f32),

time: 28.1 us -> 27.1 us (0.964)
  Pallas kernels: 27.3 us -> 26.3 us
    pallas_call x1, Pallas kernels: 26.4 us -> 25.4 us  [body(): pl.pallas_call(functools.partial(kernel, nx, ny, cells), out_shape=(pltpu...]
where the time goes in v3:
time: 27.1 us; the launch traced here: 26.9 us
  Pallas kernels  26.3 us (97%)
  between operations  0.64 us (2%)
    pallas_call x1, Pallas kernels, body(): pl.pallas_call(functools.partial(kernel, nx, ny, cells), out_shape=(pltpu...  25.4 us
    pallas_call x1, Pallas kernels, body(): pl.pallas_call(finish, out_shape=(jax.ShapeDtypeStruct(shape, f32), jax.S...  0.89 us

profile of v3, /device:TPU:0, one launch (start us, length us, event | category | flops | bytes accessed | tf_op | source)
XLA Modules:
  0.0 26.9 jit_solution(1711268897317470563)
XLA Ops:
  0.6 25.4 %shard_map.49 = (f32[4,4,64,256]{3,2,1,0:T(8,128)S(1)}, f32[3,4,64,256]{3,2,1,0:T(8,128)S(1)}, f32[9]{0:T(128)S(4)}) custom-call(f32[4,64,256]{2,1,0:T(8,128)} %rhs_hbm.1, f32[4,64,256]{2,1,0:T(8,128)} %kappa_hbm.1), custom_call_target="tpu_custom_call" | custom-call | tf_op jit(solution)/shard_map/pallas_call | solution.py:310
  26.1 0.9 %shard_map.50 = (f32[4,64,256]{2,1,0:T(8,128)}, f32[4,64,256]{2,1,0:T(8,128)}, f32[3]{0:T(128)}) custom-call(f32[9]{0:T(128)S(4)} %get-tuple-element.6.coef, f32[4,4,64,256]{3,2,1,0:T(8,128)S(1)} %get-tuple-element.7.v_ref, f32[3,4,64,256]{3,2,1,0:T(8,128)S(1)} %get-tuple-element.8.y_ref), custom_call_target="tpu_custom_call" | custom-call | tf_op jit(solution)/shard_map/pallas_call | solution.py:341

commit v4 on v3

--- a/solution.py
+++ b/solution.py
@@ -202,11 +202,11 @@
         mu.append(tile_sum(sum(v_ref[j, l] * y_ref[j, l] for l in range(layers))))
         for i in range(j + 1):
             dots[i, j] = tile_sum(sum(v_ref[i, l] * v_ref[j, l] for l in range(layers)))
-        for copy in edges[0]:
-            copy.wait_recv()
-        if relayed:
-            for copy in corners:
-                copy.start()
+        for side in range(2):
+            edges[0][1 - side].wait_recv()
+            if relayed:
+                corners[side].start()
+                corners[2 + side].start()
         for copy in faces[0]:
             copy.wait_recv()
         full = ITERS + j % 2
@@ -222,7 +222,7 @@
                 t_ref[full, l, at, :] = t_ref[full, l, at, :] - edge_in[j, 0, side, l]
         mu.append(tile_sum(sum(t_ref[full, l] * t_ref[full, l] for l in range(layers))))
         if j == ITERS - 1:
-            start_sums(mu, dots, slots, sum_send, sum_recv, me, count, ny)
+            start_sums(mu, dots, slots, sum_send, sum_recv, me, nx, ny)
         get_t = lambda l: t_ref[full, l]
         for l in range(layers):
             v = local_k(get_t, l)
@@ -255,33 +255,45 @@
     pltpu.make_async_copy(all_slots, all_slots, sum_recv).wait()
     total = jnp.sum(slots[...], axis=0)
     names = [("mu", i) for i in range(2 * ITERS)] + sorted(dots)
-    got = {name: total[:, k : k + 1] for k, name in enumerate(names)}
+    got = {
+        name: jnp.broadcast_to(total[:, k : k + 1], total.shape) for k, name in enumerate(names)
+    }
     mu = [got["mu", i] for i in range(2 * ITERS)]
     sol, res, norms = coefficients(mu, got, float(cells))
     for k, value in enumerate(norms + sol[:ITERS] + res[1:]):
         coef_ref[k] = value[0, 0]
 
 
-def start_sums(mu, dots, slots, sum_send, sum_recv, me, count, ny):
+def start_sums(mu, dots, slots, sum_send, sum_recv, me, nx, ny):
     lane = lax.broadcasted_iota(jnp.int32, (1, slots.shape[-1]), 1)
     line = jnp.zeros(lane.shape, jnp.float32)
     for k, value in enumerate(mu + [dots[name] for name in sorted(dots)]):
         line = jnp.where(lane == k, value, line)
     slots[me] = line
 
-    def send(k, carry):
-        other = lax.rem(me + k, count)
+    def send(x, y):
         pltpu.make_async_remote_copy(
             src_ref=slots.at[me],
             dst_ref=slots.at[me],
             send_sem=sum_send,
             recv_sem=sum_recv,
-            device_id=(other // ny, lax.rem(other, ny)),
+            device_id=(x, y),
             device_id_type=MESH,
         ).start()
+
+    ix, iy = lax.axis_index("gx"), lax.axis_index("gy")
+    y_at = [lax.rem(iy + k, ny) for k in range(ny)]
+
+    def send_line(k, carry):
+        x = ix + k
+        x = jnp.where(x >= nx, x - nx, x)
+        for y in y_at[1:] + y_at[:1]:
+            send(x, y)
         return carry
 
-    lax.fori_loop(1, count, send, 0)
+    lax.fori_loop(1, nx, send_line, 0)
+    for y in y_at[1:]:
+        send(ix, y)
 
 
 def finish(coef, v_ref, y_ref, sol_ref, res_ref, norms_ref):

time: 27.1 us -> 26.7 us (0.985)
  Pallas kernels: 26.3 us -> 25.9 us
    pallas_call x1, Pallas kernels: 25.4 us -> 25 us  [body(): pl.pallas_call(functools.partial(kernel, nx, ny, cells), out_shape=(pltpu...]
where the time goes in v4:
time: 26.7 us; the launch traced here: 26.5 us
  Pallas kernels  25.9 us (97%)
  between operations  0.64 us (2%)
    pallas_call x1, Pallas kernels, body(): pl.pallas_call(functools.partial(kernel, nx, ny, cells), out_shape=(pltpu...  25 us
    pallas_call x1, Pallas kernels, body(): pl.pallas_call(finish, out_shape=(jax.ShapeDtypeStruct(shape, f32), jax.S...  0.89 us

profile of v4, /device:TPU:0, one launch (start us, length us, event | category | flops | bytes accessed | tf_op | source)
XLA Modules:
  0.0 26.5 jit_solution(8825708983955300367)
XLA Ops:
  0.6 25.0 %shard_map.49 = (f32[4,4,64,256]{3,2,1,0:T(8,128)S(1)}, f32[3,4,64,256]{3,2,1,0:T(8,128)S(1)}, f32[9]{0:T(128)S(4)}) custom-call(f32[4,64,256]{2,1,0:T(8,128)} %rhs_hbm.1, f32[4,64,256]{2,1,0:T(8,128)} %kappa_hbm.1), custom_call_target="tpu_custom_call" | custom-call | tf_op jit(solution)/shard_map/pallas_call | solution.py:322
  25.6 0.9 %shard_map.50 = (f32[4,64,256]{2,1,0:T(8,128)}, f32[4,64,256]{2,1,0:T(8,128)}, f32[3]{0:T(128)}) custom-call(f32[9]{0:T(128)S(4)} %get-tuple-element.6.coef, f32[4,4,64,256]{3,2,1,0:T(8,128)S(1)} %get-tuple-element.7.v_ref, f32[3,4,64,256]{3,2,1,0:T(8,128)S(1)} %get-tuple-element.8.y_ref), custom_call_target="tpu_custom_call" | custom-call | tf_op jit(solution)/shard_map/pallas_call | solution.py:353
